TPU v7x, 32 devices: a whole 2x2x4 slice. The times are simulated.
32 devices in a mesh: groups: 2 (over y), space: 4 (over z), rhs: 4 (over x, core).
Axes of the slice: x: 2, y: 2, z: 4, core: 2. Of those that a mesh axis runs over, the one named last changes fastest.
Arguments:
- conductance: float32 [64, 1024], P(('groups', 'space')), parts along dimension 0, may hold values from 0.05 to 2
- nodata: int32 [64, 1024], P(('groups', 'space')), parts along dimension 0, may hold values 0 or 1
- ground_mask: int32 [64, 1024], P(('groups', 'space')), parts along dimension 0, may hold values 0 or 1
- ground_value: float32 [64, 1024], P(('groups', 'space')), parts along dimension 0, may hold values from 0.5 to 4
- source_mask: int32 [64, 1024], P(('groups', 'space')), parts along dimension 0, may hold values 0 or 1
- source_current: float32 [64, 1024], P(('groups', 'space')), parts along dimension 0, may hold values from 0.5 to 4
- tile_inverse: float32 [64, 8, 128, 128], P(('groups', 'space')), parts along dimension 0, may hold values from -0.04 to 8, as said below
- focal_cells: int32 [512, 2], P(('groups', 'rhs')), parts along dimension 0, may hold values from 0 to 32767
Outputs:
- solution: float32 [256, 64, 1024], P('rhs', ('groups', 'space')), parts along dimension 1
- residual: float32 [256, 64, 1024], P('rhs', ('groups', 'space')), parts along dimension 1
There are 2 independent parts, one for each index of `groups`. A program takes and returns all parts, laid end to end along the dimension named above; each array names one. Nothing has to cross between parts.
Inputs may be any that keep to these rules, and one draw needn't show every extreme that they name: `tile_inverse`: each block is symmetric positive definite.
All inputs are finite; a program needn't handle non-finite values. No bound on the sum of `nodata` or of `ground_mask` or of `source_mask` on one device may be relied on, other than what follows from the above.
Results may differ from a plain program's by a relative error of at most 0.00025.
Values sent between devices are 32-bit elements; how exact they have to be, the bound alone decides.
A program may use at most 64 MiB of HBM per device.

v0:
```python
import jax
import jax.numpy as jnp
from jax import lax
from jax.sharding import PartitionSpec as P

ITERS = 2


LEAKAGE = 0.05
FOCAL_CURRENT = 16.0


def with_halo(cells, sides, width):
    for axis, dim in sides:
        count = lax.axis_size(axis)
        ends = count - 1
        head = lax.slice_in_dim(cells, 0, width, axis=dim)
        tail = lax.slice_in_dim(cells, cells.shape[dim] - width, cells.shape[dim], axis=dim)
        cells = jnp.concatenate(
            [
                lax.ppermute(tail, axis, [(i, (i + 1) % count) for i in range(ends)]),
                cells,
                lax.ppermute(head, axis, [((i + 1) % count, i) for i in range(ends)]),
            ],
            axis=dim,
        )
    return cells


def weights_from(padded_g, padded_v, valid_mask, ground_mask, ground_value):
    centre = padded_g[1:-1, 1:-1]
    north_w = 0.5 * (centre + padded_g[:-2, 1:-1]) * valid_mask * padded_v[:-2, 1:-1]
    south_w = 0.5 * (centre + padded_g[2:, 1:-1]) * valid_mask * padded_v[2:, 1:-1]
    west_w = 0.5 * (centre + padded_g[1:-1, :-2]) * valid_mask * padded_v[1:-1, :-2]
    east_w = 0.5 * (centre + padded_g[1:-1, 2:]) * valid_mask * padded_v[1:-1, 2:]
    grounded = ground_mask.astype(jnp.float32) * ground_value
    diagonal = (
        valid_mask * (LEAKAGE + grounded) + (1.0 - valid_mask) + north_w + south_w + west_w + east_w
    )
    return (diagonal, north_w, south_w, west_w, east_w)


def stencil(padded, weights):
    diagonal, north_w, south_w, west_w, east_w = weights
    centre = padded[:, 1:-1, 1:-1]
    return (
        diagonal * centre
        - north_w * padded[:, :-2, 1:-1]
        - south_w * padded[:, 2:, 1:-1]
        - west_w * padded[:, 1:-1, :-2]
        - east_w * padded[:, 1:-1, 2:]
    )


def pad_columns(rimmed):
    return jnp.pad(rimmed, ((0, 0), (0, 0), (1, 1)))


def precondition(field_in, tile_inverse):
    pair_count, row_count, col_count = field_in.shape
    blocks = field_in.reshape(pair_count, row_count, col_count // 128, 128)
    result = jnp.einsum(
        "rcij,prcj->prci",
        tile_inverse,
        blocks,
        precision=lax.Precision.HIGHEST,
        preferred_element_type=jnp.float32,
    )
    return result.reshape(pair_count, row_count, col_count)


def inner_sum(first, second):
    return jnp.sum(first * second, axis=(1, 2))


def search_image(precond, weights):
    rimmed = with_halo(precond, (("space", 1),), 1)
    return stencil(pad_columns(rimmed), weights)


def paired_sums(residual, precond, image):
    return lax.psum((inner_sum(residual, precond), inner_sum(image, precond)), "space")


def on_device(
    conductance,
    nodata,
    ground_mask,
    ground_value,
    source_mask,
    source_current,
    tile_inverse,
    focal_cells,
):
    valid_mask = (1 - nodata).astype(jnp.float32)
    active = conductance * valid_mask
    stacked = jnp.stack([active, valid_mask])
    rimmed = with_halo(stacked, (("space", 1),), 1)
    rimmed = pad_columns(rimmed)
    weights = weights_from(rimmed[0], rimmed[1], valid_mask, ground_mask, ground_value)
    row_count, col_count = conductance.shape
    offset = lax.axis_index("space") * (row_count * col_count)
    cell_ids = offset + jnp.arange(row_count * col_count, dtype=jnp.int32)
    onehot = (cell_ids[None, :] == focal_cells[:, 0:1]).astype(jnp.float32) - (
        cell_ids[None, :] == focal_cells[:, 1:2]
    ).astype(jnp.float32)
    onehot = onehot.reshape(focal_cells.shape[0], row_count, col_count)
    background = source_mask.astype(jnp.float32) * source_current
    right_side = background[None] + FOCAL_CURRENT * onehot
    solution = jnp.zeros_like(right_side)
    residual = right_side
    precond = precondition(residual, tile_inverse)
    image = search_image(precond, weights)
    gamma_now, curvature = paired_sums(residual, precond, image)
    step_len = gamma_now / curvature
    direction = precond
    along = image
    for iteration in range(ITERS):
        solution = solution + step_len[:, None, None] * direction
        residual = residual - step_len[:, None, None] * along
        if iteration + 1 < ITERS:
            precond = precondition(residual, tile_inverse)
            image = search_image(precond, weights)
            gamma_next, curvature = paired_sums(residual, precond, image)
            ratio_next = gamma_next / gamma_now
            step_len = gamma_next / (curvature - ratio_next * gamma_next / step_len)
            direction = precond + ratio_next[:, None, None] * direction
            along = image + ratio_next[:, None, None] * along
            gamma_now = gamma_next
    return (solution, residual)


def solution(mesh):
    return jax.shard_map(
        on_device,
        mesh=mesh,
        in_specs=(
            P(("groups", "space"), None),
            P(("groups", "space"), None),
            P(("groups", "space"), None),
            P(("groups", "space"), None),
            P(("groups", "space"), None),
            P(("groups", "space"), None),
            P(("groups", "space"), None, None, None),
            P(("groups", "rhs"), None),
        ),
        out_specs=(P("rhs", ("groups", "space"), None), P("rhs", ("groups", "space"), None)),
        check_vma=False,
    )
```

profile of v0, /device:TPU:0, one launch (start us, length us, event | category | flops | bytes accessed | tf_op | source)
XLA Modules:
  0.0 105.8 jit_solution(10879014617259955688)
XLA Ops:
  2.2 5.0 %collective-permute-start = (f32[2,1,1024]{2,1,0:T(1,128)S(1)}, f32[2,1,1024]{2,1,0:T(1,128)S(1)}, u32[]{:S(2)}, u32[]{:S(2)}) collective-permute-start(f32[2,1,1024]{2,1,0:T(1,128)S(1)} %get-tuple-element.23), channel_id=1, source_target_pairs={{0,4},{4,8},{8,12},{1,5},{5,9},{9,13},{2,6},{6,10},{10,14},{3,7},{... | collective-permute-start | bytes 24584 | tf_op jit(solution)/shard_map/ppermute | solution.py:21
  7.2 1.3 %collective-permute-start.1 = (f32[2,1,1024]{2,1,0:T(1,128)S(1)}, f32[2,1,1024]{2,1,0:T(1,128)S(1)}, u32[]{:S(2)}, u32[]{:S(2)}) collective-permute-start(f32[2,1,1024]{2,1,0:T(1,128)S(1)} %get-tuple-element.24), channel_id=1, source_target_pairs={{4,0},{8,4},{12,8},{5,1},{9,5},{13,9},{6,2},{10,6},{14,10},{7,3},{... | collective-permute-start | bytes 24584 | tf_op jit(solution)/shard_map/ppermute | solution.py:23
  10.0 10.3 %multiply_reduce_fusion.3 = (f32[64]{0:T(128)S(1)}, f32[64,8,8,128]{3,0,2,1:T(8,128)S(1)}) fusion(s32[8,8,128]{2,1,0:T(8,128)S(1)} %add_add_fusion.2, f32[8,8,128]{2,1,0:T(8,128)S(1)} %copy.12, s32[64]{0:T(128)S(1)} %get-tuple-element.26, s32[64]{0:T(128)S(1)} %get-tuple-element.25, f32[8,8,128,128]{3,2,1,0:T(8,128)} %param.14), kind=kOutput, calls=%fused_computation.35 | convolution fusion | flops 813694912 | bytes 6357760 | tf_op jit(solution)/shard_map/rcij,prcj->prci/dot_general | solution.py:62
  20.4 2.5 %copy.13 = f32[64,8,8,128]{3,2,1,0:T(8,128)} copy(f32[64,8,8,128]{3,0,2,1:T(8,128)S(1)} %get-tuple-element.28) | data formatting | bytes 4194304 | tf_op jit(solution)/shard_map/rcij,prcj->prci/transpose | solution.py:62
  22.9 1.7 %reshape.74 = f32[64,8,1024]{2,1,0:T(8,128)S(1)} reshape(f32[64,8,8,128]{3,2,1,0:T(8,128)} %copy.13) | data formatting | bytes 4194304 | tf_op jit(solution)/shard_map/reshape | solution.py:69
  25.0 4.6 %collective-permute-start.2 = (f32[64,1,1024]{2,1,0:T(1,128)S(1)}, f32[64,1,1024]{2,1,0:T(1,128)S(1)}, u32[]{:S(2)}, u32[]{:S(2)}) collective-permute-start(f32[64,1,1024]{2,1,0:T(1,128)S(1)} %get-tuple-element.19), channel_id=1, source_target_pairs={{0,4},{4,8},{8,12},{1,5},{5,9},{9,13},{2,6},{6,10},{10,14},{3,7},{... | collective-permute-start | bytes 786440 | tf_op jit(solution)/shard_map/ppermute | solution.py:21
  31.2 3.3 %collective-permute-done.2 = f32[64,1,1024]{2,1,0:T(1,128)S(1)} collective-permute-done((f32[64,1,1024]{2,1,0:T(1,128)S(1)}, f32[64,1,1024]{2,1,0:T(1,128)S(1)}, u32[]{:S(2)}, u32[]{:S(2)}) %collective-permute-start.2) | collective-permute-done | bytes 262176 | tf_op jit(solution)/shard_map/ppermute | solution.py:21
  34.5 4.1 %collective-permute-done.3 = f32[64,1,1024]{2,1,0:T(1,128)S(1)} collective-permute-done((f32[64,1,1024]{2,1,0:T(1,128)S(1)}, f32[64,1,1024]{2,1,0:T(1,128)S(1)}, u32[]{:S(2)}, u32[]{:S(2)}) %collective-permute-start.3) | collective-permute-done | bytes 262176 | tf_op jit(solution)/shard_map/ppermute | solution.py:23
  38.6 3.4 %select_maximum_fusion.2 = f32[64,10,1026]{2,1,0:T(8,128)S(1)} fusion(f32[64,1,1024]{2,1,0:T(1,128)S(1)} %collective-permute-done.3, f32[64,8,1024]{2,1,0:T(8,128)S(1)} %reshape.74, f32[64,1,1024]{2,1,0:T(1,128)S(1)} %collective-permute-done.2), kind=kLoop, calls=%fused_computation.4 | loop fusion | flops 5253120 | bytes 5248000 | tf_op jit(solution)/shard_map/concatenate | solution.py:19
  42.0 3.0 %multiply_reduce_fusion.2 = (f32[64]{0:T(128)S(1)}, f32[64,8,1024]{2,1,0:T(8,128)}) fusion(f32[64,8,1024]{2,1,0:T(8,128)S(1)} %reshape.74, f32[64,10,1026]{2,1,0:T(8,128)S(1)} %select_maximum_fusion.2, f32[8,1024]{1,0:T(8,128)S(1)} %get-tuple-element.16, f32[8,1024]{1,0:T(8,128)S(1)} %get-tuple-element.15, f32[64,1,1024]{2,1,0:T(1,128)S(1)} %collective-permute-done.3, ...), kind=kLoop, calls=%fused_computation.34 | loop fusion | flops 6815680 | bytes 9076992 | tf_op jit(solution)/shard_map/reduce_sum | solution.py:73
  45.0 10.1 %all-reduce.4 = (f32[64]{0:T(128)S(1)}, f32[64]{0:T(128)S(1)}) all-reduce(f32[64]{0:T(128)S(1)} %get-tuple-element.27, f32[64]{0:T(128)S(1)} %get-tuple-element.10), channel_id=1, replica_groups=mesh['groups'=2,'space'=4,'rhs'=4] {'space'}, use_global_device_ids=true, to_apply=%region_1.2 | all-reduce | flops 128 | bytes 1024 | tf_op jit(solution)/shard_map/psum | solution.py:82
  55.1 2.4 %fusion.22 = f32[64,8,8,128]{3,1,2,0:T(8,128)S(1)} fusion(f32[64,8,1024]{2,1,0:T(8,128)} %get-tuple-element.11, s32[8,1024]{1,0:T(8,128)S(1)} %add_add_fusion, f32[8,1024]{1,0:T(8,128)S(1)} %convert_multiply_fusion, f32[64]{0:T(128)S(1)} %div.12, s32[64]{0:T(128)S(1)} %get-tuple-element.26, s32[64]{0:T(128)S(1)} %get-tuple-element.25), kind=kLoop, calls=%fused_computation.42 | loop fusion | flops 4718592 | bytes 4260608 | tf_op jit(solution)/shard_map/reshape | solution.py:61
  57.9 8.3 %fusion.18 = f32[64,8,8,128]{3,0,2,1:T(8,128)S(1)} fusion(f32[8,8,128,128]{3,2,1,0:T(8,128)S(1)} %copy-done.4, f32[64,8,8,128]{3,1,2,0:T(8,128)S(1)} %fusion.22), kind=kOutput, calls=%fused_computation.40 | convolution fusion | flops 805306368 | bytes 8388608 | tf_op jit(solution)/shard_map/rcij,prcj->prci/dot_general | solution.py:62
  66.2 2.5 %copy.15 = f32[64,8,8,128]{3,2,1,0:T(8,128)} copy(f32[64,8,8,128]{3,0,2,1:T(8,128)S(1)} %fusion.18) | data formatting | bytes 4194304 | tf_op jit(solution)/shard_map/rcij,prcj->prci/transpose | solution.py:62
  68.8 1.7 %reshape.76 = f32[64,8,1024]{2,1,0:T(8,128)S(1)} reshape(f32[64,8,8,128]{3,2,1,0:T(8,128)} %copy.15) | data formatting | bytes 4194304 | tf_op jit(solution)/shard_map/reshape | solution.py:69
  70.8 2.5 %collective-permute-start.4 = (f32[64,1,1024]{2,1,0:T(1,128)S(1)}, f32[64,1,1024]{2,1,0:T(1,128)S(1)}, u32[]{:S(2)}, u32[]{:S(2)}) collective-permute-start(f32[64,1,1024]{2,1,0:T(1,128)S(1)} %get-tuple-element.17), channel_id=1, source_target_pairs={{0,4},{4,8},{8,12},{1,5},{5,9},{9,13},{2,6},{6,10},{10,14},{3,7},{... | collective-permute-start | bytes 786440 | tf_op jit(solution)/shard_map/ppermute | solution.py:21
  73.4 1.6 %collective-permute-start.5 = (f32[64,1,1024]{2,1,0:T(1,128)S(1)}, f32[64,1,1024]{2,1,0:T(1,128)S(1)}, u32[]{:S(2)}, u32[]{:S(2)}) collective-permute-start(f32[64,1,1024]{2,1,0:T(1,128)S(1)} %get-tuple-element.18), channel_id=1, source_target_pairs={{4,0},{8,4},{12,8},{5,1},{9,5},{13,9},{6,2},{10,6},{14,10},{7,3},{... | collective-permute-start | bytes 786440 | tf_op jit(solution)/shard_map/ppermute | solution.py:23
  75.0 2.2 %collective-permute-done.4 = f32[64,1,1024]{2,1,0:T(1,128)S(1)} collective-permute-done((f32[64,1,1024]{2,1,0:T(1,128)S(1)}, f32[64,1,1024]{2,1,0:T(1,128)S(1)}, u32[]{:S(2)}, u32[]{:S(2)}) %collective-permute-start.4) | collective-permute-done | bytes 262176 | tf_op jit(solution)/shard_map/ppermute | solution.py:21
  77.2 4.6 %collective-permute-done.5 = f32[64,1,1024]{2,1,0:T(1,128)S(1)} collective-permute-done((f32[64,1,1024]{2,1,0:T(1,128)S(1)}, f32[64,1,1024]{2,1,0:T(1,128)S(1)}, u32[]{:S(2)}, u32[]{:S(2)}) %collective-permute-start.5) | collective-permute-done | bytes 262176 | tf_op jit(solution)/shard_map/ppermute | solution.py:23
  81.8 3.4 %select_maximum_fusion = f32[64,10,1026]{2,1,0:T(8,128)S(1)} fusion(f32[64,1,1024]{2,1,0:T(1,128)S(1)} %collective-permute-done.5, f32[64,8,1024]{2,1,0:T(8,128)S(1)} %reshape.76, f32[64,1,1024]{2,1,0:T(1,128)S(1)} %collective-permute-done.4), kind=kLoop, calls=%fused_computation.2 | loop fusion | flops 5253120 | bytes 5248000 | tf_op jit(solution)/shard_map/concatenate | solution.py:19
  85.2 3.4 %multiply_reduce_fusion = (f32[64]{0:T(128)S(1)}, f32[64]{0:T(128)S(1)}) fusion(f32[64,8,1024]{2,1,0:T(8,128)S(1)} %reshape.76, f32[64,10,1026]{2,1,0:T(8,128)S(1)} %select_maximum_fusion, f32[8,1024]{1,0:T(8,128)S(1)} %get-tuple-element.16, f32[8,1024]{1,0:T(8,128)S(1)} %get-tuple-element.15, f32[64,1,1024]{2,1,0:T(1,128)S(1)} %collective-permute-done.5, ...), kind=kLoop, calls=%fused_computation.31 | loop fusion | flops 12582784 | bytes 9143552 | tf_op jit(solution)/shard_map/reduce_sum | solution.py:73
  88.6 8.4 %all-reduce.3 = (f32[64]{0:T(128)S(1)}, f32[64]{0:T(128)S(1)}) all-reduce(f32[64]{0:T(128)S(1)} %get-tuple-element.3, f32[64]{0:T(128)S(1)} %get-tuple-element.2), channel_id=1, replica_groups=mesh['groups'=2,'space'=4,'rhs'=4] {'space'}, use_global_device_ids=true, to_apply=%region_5.6 | all-reduce | flops 128 | bytes 1024 | tf_op jit(solution)/shard_map/psum | solution.py:82
  97.0 3.5 %multiply_add_fusion = f32[64,8,1024]{2,1,0:T(8,128)} fusion(f32[64,8,1024]{2,1,0:T(8,128)S(1)} %reshape.76, f32[64,8,1024]{2,1,0:T(8,128)} %copy-done, f32[64]{0:T(128)S(1)} %get-tuple-element.9, f32[64]{0:T(128)S(1)} %get-tuple-element.8, f32[64]{0:T(128)S(1)} %div.12), kind=kLoop, calls=%fused_computation.30 | loop fusion | flops 2621440 | bytes 6292224 | tf_op jit(solution)/shard_map/add | solution.py:119
  100.5 5.3 %multiply_subtract_fusion = f32[64,8,1024]{2,1,0:T(8,128)} fusion(f32[64,8,1024]{2,1,0:T(8,128)} %get-tuple-element.11, f32[64]{0:T(128)S(1)} %get-tuple-element.9, f32[64]{0:T(128)S(1)} %get-tuple-element.8, s32[8,1024]{1,0:T(8,128)S(1)} %add_add_fusion, f32[8,1024]{1,0:T(8,128)S(1)} %convert_multiply_fusion, f32[64]{0:T(128)S(1)} %div.12, ...), kind=kLoop, calls=%fused_computation.29 | loop fusion | flops 12582912 | bytes 11240704 | tf_op jit(solution)/shard_map/sub | solution.py:120
  (34 shorter events, 5.8 us)
Async XLA Ops:
  2.2 28.7 %collective-permute-start = (f32[2,1,1024]{2,1,0:T(1,128)S(1)}, f32[2,1,1024]{2,1,0:T(1,128)S(1)}, u32[]{:S(2)}, u32[]{:S(2)}) collective-permute-start(f32[2,1,1024]{2,1,0:T(1,128)S(1)} %get-tuple-element.23), channel_id=1, source_target_pairs={{0,4},{4,8},{8,12},{1,5},{5,9},{9,13},{2,6},{6,10},{10,14},{3,7},{... | collective-permute-start | bytes 24584 | tf_op jit(solution)/shard_map/ppermute | solution.py:21
  7.2 23.7 %collective-permute-start.1 = (f32[2,1,1024]{2,1,0:T(1,128)S(1)}, f32[2,1,1024]{2,1,0:T(1,128)S(1)}, u32[]{:S(2)}, u32[]{:S(2)}) collective-permute-start(f32[2,1,1024]{2,1,0:T(1,128)S(1)} %get-tuple-element.24), channel_id=1, source_target_pairs={{4,0},{8,4},{12,8},{5,1},{9,5},{13,9},{6,2},{10,6},{14,10},{7,3},{... | collective-permute-start | bytes 24584 | tf_op jit(solution)/shard_map/ppermute | solution.py:23
  22.9 8.2 %copy-start.5 = (s32[8,1024]{1,0:T(8,128)S(1)}, s32[8,1024]{1,0:T(8,128)}, u32[]{:S(2)}) copy-start(s32[8,1024]{1,0:T(8,128)} %param.9) | copy-start | bytes 98308
  22.9 8.2 %copy-start.6 = (f32[8,1024]{1,0:T(8,128)S(1)}, f32[8,1024]{1,0:T(8,128)}, u32[]{:S(2)}) copy-start(f32[8,1024]{1,0:T(8,128)} %param.11) | copy-start | bytes 98308
  22.9 8.2 %copy-start.7 = (s32[8,1024]{1,0:T(8,128)S(1)}, s32[8,1024]{1,0:T(8,128)}, u32[]{:S(2)}) copy-start(s32[8,1024]{1,0:T(8,128)} %param.10) | copy-start | bytes 98308
  24.6 17.4 %copy-start = (f32[64,8,1024]{2,1,0:T(8,128)}, f32[64,8,1024]{2,1,0:T(8,128)S(1)}, u32[]{:S(2)}) copy-start(f32[64,8,1024]{2,1,0:T(8,128)S(1)} %reshape.74) | copy-start | bytes 6291460
  25.0 9.5 %collective-permute-start.2 = (f32[64,1,1024]{2,1,0:T(1,128)S(1)}, f32[64,1,1024]{2,1,0:T(1,128)S(1)}, u32[]{:S(2)}, u32[]{:S(2)}) collective-permute-start(f32[64,1,1024]{2,1,0:T(1,128)S(1)} %get-tuple-element.19), channel_id=1, source_target_pairs={{0,4},{4,8},{8,12},{1,5},{5,9},{9,13},{2,6},{6,10},{10,14},{3,7},{... | collective-permute-start | bytes 786440 | tf_op jit(solution)/shard_map/ppermute | solution.py:21
  29.5 9.1 %collective-permute-start.3 = (f32[64,1,1024]{2,1,0:T(1,128)S(1)}, f32[64,1,1024]{2,1,0:T(1,128)S(1)}, u32[]{:S(2)}, u32[]{:S(2)}) collective-permute-start(f32[64,1,1024]{2,1,0:T(1,128)S(1)} %get-tuple-element.20), channel_id=1, source_target_pairs={{4,0},{8,4},{12,8},{5,1},{9,5},{13,9},{6,2},{10,6},{14,10},{7,3},{... | collective-permute-start | bytes 786440 | tf_op jit(solution)/shard_map/ppermute | solution.py:23
  55.1 2.8 %copy-start.4 = (f32[8,8,128,128]{3,2,1,0:T(8,128)S(1)}, f32[8,8,128,128]{3,2,1,0:T(8,128)}, u32[]{:S(2)}) copy-start(f32[8,8,128,128]{3,2,1,0:T(8,128)} %param.14) | copy-start | bytes 12582916
  70.8 6.4 %collective-permute-start.4 = (f32[64,1,1024]{2,1,0:T(1,128)S(1)}, f32[64,1,1024]{2,1,0:T(1,128)S(1)}, u32[]{:S(2)}, u32[]{:S(2)}) collective-permute-start(f32[64,1,1024]{2,1,0:T(1,128)S(1)} %get-tuple-element.17), channel_id=1, source_target_pairs={{0,4},{4,8},{8,12},{1,5},{5,9},{9,13},{2,6},{6,10},{10,14},{3,7},{... | collective-permute-start | bytes 786440 | tf_op jit(solution)/shard_map/ppermute | solution.py:21
  73.4 11.8 %copy-start.3 = (f32[64,8,1024]{2,1,0:T(8,128)S(1)}, f32[64,8,1024]{2,1,0:T(8,128)}, u32[]{:S(2)}) copy-start(f32[64,8,1024]{2,1,0:T(8,128)} %get-tuple-element.11) | copy-start | bytes 6291460
  73.4 8.4 %collective-permute-start.5 = (f32[64,1,1024]{2,1,0:T(1,128)S(1)}, f32[64,1,1024]{2,1,0:T(1,128)S(1)}, u32[]{:S(2)}, u32[]{:S(2)}) collective-permute-start(f32[64,1,1024]{2,1,0:T(1,128)S(1)} %get-tuple-element.18), channel_id=1, source_target_pairs={{4,0},{8,4},{12,8},{5,1},{9,5},{13,9},{6,2},{10,6},{14,10},{7,3},{... | collective-permute-start | bytes 786440 | tf_op jit(solution)/shard_map/ppermute | solution.py:23
  85.1 3.4 %copy-start.1 = (f32[64,10,1026]{2,1,0:T(8,128)}, f32[64,10,1026]{2,1,0:T(8,128)S(1)}, u32[]{:S(2)}) copy-start(f32[64,10,1026]{2,1,0:T(8,128)S(1)} %select_maximum_fusion) | copy-start | bytes 7879684
  97.0 3.5 %copy-start.2 = (f32[64,10,1026]{2,1,0:T(8,128)S(1)}, f32[64,10,1026]{2,1,0:T(8,128)}, u32[]{:S(2)}) copy-start(f32[64,10,1026]{2,1,0:T(8,128)} %copy-done.1) | copy-start | bytes 7879684
where the time goes:
time: 106 us
  other arithmetic  27 us (25%)
  matrix products  18.6 us (18%)
  blocking collectives  18.5 us (17%)
  starting transfers between devices  16.3 us (15%)
  waiting for transfers between devices  14.2 us (13%)
  local copies, waits for them, and re-layouts  10.4 us (10%)
    dot_general x2, matrix products, precondition(): jnp.einsum('rcij,prcj->prci', tile_inverse, blocks, precision=lax.Precisi...  18.6 us
    psum x2, blocking collectives, paired_sums(): lax.psum((inner_sum(residual, precond), inner_sum(image, precond)), 'space')  18.5 us
    ppermute x3, starting transfers between devices, with_halo(): lax.ppermute(tail, axis, [(i, (i + 1) % count) for i in range(ends)])  12.1 us
    ppermute x3, waiting for transfers between devices, with_halo(): lax.ppermute(head, axis, [((i + 1) % count, i) for i in range(ends)])  8.68 us
    concatenate x3, other arithmetic, with_halo(): jnp.concatenate([lax.ppermute(tail, axis, [(i, (i + 1) % count) for i in...  6.85 us
    reduce_sum x2, other arithmetic, inner_sum(): return jnp.sum(first * second, axis=(1, 2))  6.4 us
    ppermute x3, waiting for transfers between devices, with_halo(): lax.ppermute(tail, axis, [(i, (i + 1) % count) for i in range(ends)])  5.49 us
    sub x1, other arithmetic, on_device(): residual = residual - step_len[:, None, None] * along  5.27 us
  transfers between devices with their start and end apart: 6, of which 4 were waited for; matrix products, arithmetic and copies ran while one was open for 16% of the time, Pallas kernels for 0%

commit v1 on v0

v1 whole, which is shorter than its diff:
```python
import functools

import jax
import jax.numpy as jnp
from jax import lax
from jax.experimental import pallas as pl
from jax.experimental.pallas import tpu as pltpu
from jax.sharding import PartitionSpec as P

LEAKAGE = 0.05
FOCAL_CURRENT = 16.0
LANES = 128
EXTRA = 8
F32 = jnp.float32
BF16 = jnp.bfloat16


def fold(x):
    out = x[:, :LANES]
    for c in range(1, x.shape[1] // LANES):
        out = out + x[:, c * LANES:(c + 1) * LANES]
    return out


def krylov_kernel(
    count, cond_ref, nodata_ref, gmask_ref, gval_ref, smask_ref, scur_ref, t_ref, focal_ref,
    q_ref, w_ref, z_ref, y_ref, coef_ref,
    r0_ref, thl_ref, wts_ref, qhalo_ref, zhalo_ref, msg_ref, got_ref, acc_ref, stat_ref, all_ref,
    send1, recv1, send2, recv2, send3, recv3,
):
    rows, cols = cond_ref.shape
    tiles = cols // LANES
    pairs = focal_ref.shape[0]
    ext = pairs + EXTRA
    groups = ext // 8
    me = lax.axis_index("space")
    last = count - 1

    barrier = pltpu.get_barrier_semaphore()
    for off in range(1, count):
        pl.semaphore_signal(
            barrier, inc=1, device_id={"space": lax.rem(me + off, count)},
            device_id_type=pl.DeviceIdType.MESH,
        )

    valid = (1 - nodata_ref[...]).astype(F32)
    active = cond_ref[...] * valid
    grounded = gmask_ref[...].astype(F32) * gval_ref[...]
    background = smask_ref[...].astype(F32) * scur_ref[...]

    def set_weights(up_a, up_v, down_a, down_v):
        lane = lax.broadcasted_iota(jnp.int32, (rows, cols), 1)
        zero = jnp.zeros((rows, cols), F32)
        row = lax.broadcasted_iota(jnp.int32, (rows, cols), 0)

        def edge(a, v):
            return 0.5 * (active + a) * valid * v

        def west(x):
            return jnp.where(lane == 0, zero, pltpu.roll(x, 1, 1))

        def east(x):
            return jnp.where(lane == cols - 1, zero, pltpu.roll(x, cols - 1, 1))

        def north(x, h):
            return jnp.where(row == 0, jnp.broadcast_to(h, x.shape), pltpu.roll(x, 1, 0))

        def south(x, h):
            return jnp.where(row == rows - 1, jnp.broadcast_to(h, x.shape), pltpu.roll(x, rows - 1, 0))

        nw = edge(north(active, up_a), north(valid, up_v))
        sw = edge(south(active, down_a), south(valid, down_v))
        ww = edge(west(active), west(valid))
        ew = edge(east(active), east(valid))
        dg = valid * (LEAKAGE + grounded) + (1.0 - valid) + nw + sw + ww + ew
        for r in range(rows):
            for i, x in enumerate((dg, nw, sw, ww, ew)):
                wts_ref[r, i:i + 1, :] = x[r:r + 1, :]

    none = jnp.zeros((1, cols), F32)
    set_weights(none, none, none, none)

    acc_ref[...] = jnp.zeros(acc_ref.shape, F32)
    fa = jnp.concatenate([focal_ref[:, 0:1], jnp.full((EXTRA, 1), -1, jnp.int32)], 0)
    fb = jnp.concatenate([focal_ref[:, 1:2], jnp.full((EXTRA, 1), -1, jnp.int32)], 0)

    for r in range(rows):
        ids = (me * rows + r) * cols + lax.broadcasted_iota(jnp.int32, (ext, cols), 1)
        onehot = (ids == fa).astype(F32) - (ids == fb).astype(F32)
        r0_ref[r] = background[r:r + 1, :] + FOCAL_CURRENT * onehot

    def precond_row(src, dst, r, split):
        for c in range(tiles):
            cut = slice(c * LANES, (c + 1) * LANES)
            if split:
                t = t_ref[r, c]
                thi = t.astype(BF16)
                thl_ref[r, c, :, :LANES] = thi
                thl_ref[r, c, :, LANES:] = (t - thi.astype(F32)).astype(BF16)
            x = src[r, :, cut]
            hi = x.astype(BF16).astype(F32)
            lhs = jnp.concatenate([hi, x - hi], 0).astype(BF16)
            o = jnp.dot(lhs, thl_ref[r, c], preferred_element_type=F32)
            dst[r, :, cut] = o[:ext, :LANES] + (o[:ext, LANES:] + (o[ext:, :LANES] + o[ext:, LANES:]))

    def precond_inner(src, dst, split):
        def body(r, carry):
            precond_row(src, dst, r, split)
            return carry
        lax.fori_loop(1, rows - 1, body, 0)

    def stencil_group(src, dst, r, no_ref, no_i, so_ref, so_i, left, base):
        def body(g, carry):
            s = pl.ds(pl.multiple_of(g * 8, 8), 8)
            ce = src[r, s, :]
            out = (
                wts_ref[r, 0:1, :] * ce
                - wts_ref[r, 1:2, :] * no_ref[no_i, s, :]
                - wts_ref[r, 2:3, :] * so_ref[so_i, s, :]
                - wts_ref[r, 3:4, :] * pltpu.roll(ce, 1, 1)
                - wts_ref[r, 4:5, :] * pltpu.roll(ce, cols - 1, 1)
            )
            dst[r, s, :] = out
            acc_ref[base, s, :] += fold(left[r, s, :] * ce)
            acc_ref[base + 1, s, :] += fold(ce * out)
            return carry
        lax.fori_loop(0, groups, body, 0)

    def stencil_inner(src, dst, left, base):
        def body(r, carry):
            stencil_group(src, dst, r, src, r - 1, src, r + 1, left, base)
            return carry
        lax.fori_loop(1, rows - 1, body, 0)

    def stencil_ends(src, dst, halo, left, base):
        stencil_group(src, dst, 0, halo, 0, src, 1, left, base)
        stencil_group(src, dst, rows - 1, src, rows - 2, halo, 1, left, base)

    def side_copy(src, dst, ssem, rsem, side):
        return pltpu.make_async_remote_copy(
            src_ref=src.at[side], dst_ref=dst.at[1 - side],
            send_sem=ssem.at[side], recv_sem=rsem.at[1 - side],
            device_id={"space": me - 1 if side == 0 else me + 1},
            device_id_type=pl.DeviceIdType.MESH,
        )

    has = (me > 0, me < last)

    precond_row(r0_ref, q_ref, 0, True)
    precond_row(r0_ref, q_ref, rows - 1, True)

    tile_a = lax.shift_right_logical(fa[:pairs] & (cols - 1), 7)
    tile_b = lax.shift_right_logical(fb[:pairs] & (cols - 1), 7)
    for side, r in ((0, 0), (1, rows - 1)):
        va = q_ref[r, :pairs, 0:LANES]
        vb = va
        for c in range(1, tiles):
            x = q_ref[r, :pairs, c * LANES:(c + 1) * LANES]
            va = jnp.where(tile_a == c, x, va)
            vb = jnp.where(tile_b == c, x, vb)
        msg_ref[side, 0:pairs, :] = va
        msg_ref[side, pairs:2 * pairs, :] = vb
        for c in range(tiles):
            cut = slice(c * LANES, (c + 1) * LANES)
            at = 2 * pairs + c
            msg_ref[side, at:at + 1, :] = q_ref[r, pairs:pairs + 1, cut]
            msg_ref[side, at + tiles:at + tiles + 1, :] = active[r:r + 1, cut]
            msg_ref[side, at + 2 * tiles:at + 2 * tiles + 1, :] = valid[r:r + 1, cut]

    pl.semaphore_wait(barrier, last)
    for side in range(2):
        @pl.when(has[side])
        def _():
            side_copy(msg_ref, got_ref, send1, recv1, side).start()

        @pl.when(jnp.logical_not(has[side]))
        def _():
            got_ref[side] = jnp.zeros(got_ref.shape[1:], F32)
            zhalo_ref[side] = jnp.zeros(zhalo_ref.shape[1:], F32)

    precond_inner(r0_ref, q_ref, True)
    stencil_inner(q_ref, w_ref, r0_ref, 0)
    precond_inner(w_ref, z_ref, False)

    def done(src, dst, ssem, rsem):
        for side in range(2):
            @pl.when(has[side])
            def _():
                side_copy(src, dst, ssem, rsem, side).wait_send()
                pltpu.make_async_remote_copy(
                    src_ref=src.at[1 - side], dst_ref=dst.at[side],
                    send_sem=ssem.at[1 - side], recv_sem=rsem.at[side],
                    device_id={"space": me - 1 if side == 0 else me + 1},
                    device_id_type=pl.DeviceIdType.MESH,
                ).wait_recv()

    done(msg_ref, got_ref, send1, recv1)

    def row_of(side, base):
        return jnp.concatenate([got_ref[side, base + c:base + c + 1, :] for c in range(tiles)], 1)

    a_at, v_at = 2 * pairs + tiles, 2 * pairs + 2 * tiles
    set_weights(row_of(0, a_at), row_of(0, v_at), row_of(1, a_at), row_of(1, v_at))
    for side in range(2):
        va = got_ref[side, 0:pairs, :]
        vb = got_ref[side, pairs:2 * pairs, :]
        for c in range(tiles):
            cut = slice(c * LANES, (c + 1) * LANES)
            common = got_ref[side, 2 * pairs + c:2 * pairs + c + 1, :]
            qhalo_ref[side, 0:pairs, cut] = jnp.where(
                tile_a == c, va, jnp.where(tile_b == c, vb, jnp.broadcast_to(common, va.shape))
            )
            qhalo_ref[side, pairs:ext, cut] = jnp.broadcast_to(common, (EXTRA, LANES))

    stencil_ends(q_ref, w_ref, qhalo_ref, r0_ref, 0)
    precond_row(w_ref, z_ref, 0, False)
    precond_row(w_ref, z_ref, rows - 1, False)

    def zcopy(side):
        r = 0 if side == 0 else rows - 1
        return pltpu.make_async_remote_copy(
            src_ref=z_ref.at[r], dst_ref=zhalo_ref.at[1 - side],
            send_sem=send2.at[side], recv_sem=recv2.at[1 - side],
            device_id={"space": me - 1 if side == 0 else me + 1},
            device_id_type=pl.DeviceIdType.MESH,
        )

    def zarrive(side):
        return pltpu.make_async_remote_copy(
            src_ref=z_ref.at[0], dst_ref=zhalo_ref.at[side],
            send_sem=send2.at[1 - side], recv_sem=recv2.at[side],
            device_id={"space": me - 1 if side == 0 else me + 1},
            device_id_type=pl.DeviceIdType.MESH,
        )

    for side in range(2):
        @pl.when(has[side])
        def _():
            zcopy(side).start()

    stencil_inner(z_ref, y_ref, w_ref, 2)

    for side in range(2):
        @pl.when(has[side])
        def _():
            zarrive(side).wait_recv()

    stencil_ends(z_ref, y_ref, zhalo_ref, w_ref, 2)

    lane = lax.broadcasted_iota(jnp.int32, (LANES, LANES), 1)
    table = jnp.zeros((LANES, LANES), F32)
    pad = jnp.zeros((LANES - pairs, 1), F32)
    for i in range(4):
        col = jnp.concatenate([jnp.sum(acc_ref[i, :pairs, :], 1, keepdims=True), pad], 0)
        table = jnp.where(lane == i, jnp.broadcast_to(col, table.shape), table)
    mine = table.T[0:8, :]
    stat_ref[...] = mine

    def stat_copy(slot, peer, k):
        return pltpu.make_async_remote_copy(
            src_ref=stat_ref, dst_ref=all_ref.at[slot],
            send_sem=send3.at[k], recv_sem=recv3.at[k],
            device_id={"space": peer}, device_id_type=pl.DeviceIdType.MESH,
        )

    for k in range(1, count):
        stat_copy(k - 1, lax.rem(me + k, count), k - 1).start()
    for side in range(2):
        @pl.when(has[side])
        def _():
            zcopy(side).wait_send()
    for k in range(1, count):
        stat_copy(k - 1, lax.rem(me + k, count), k - 1).wait()
    total = mine
    for k in range(1, count):
        total = total + all_ref[k - 1]
    back = jnp.concatenate([total, jnp.zeros((LANES - 8, LANES), F32)], 0).T
    gamma0, kappa, mu, nu = (back[:pairs, i:i + 1] for i in range(4))
    a0 = gamma0 / kappa
    gamma1 = a0 * a0 * mu - gamma0
    beta = gamma1 / gamma0
    a1 = gamma1 / (kappa - 2.0 * a0 * mu + a0 * a0 * nu - beta * gamma1 / a0)
    first = a0 + a1 * (1.0 + beta)
    lane_p = lax.broadcasted_iota(jnp.int32, (pairs, LANES), 1)
    coef_ref[...] = jnp.where(lane_p < LANES // 2, first, a0 * a1)


def combine_kernel(smask_ref, scur_ref, focal_ref, coef_ref, q_ref, w_ref, z_ref, y_ref, sol_ref, res_ref):
    rows, block, cols = q_ref.shape
    me = lax.axis_index("space")
    background = smask_ref[...].astype(F32) * scur_ref[...]
    fa, fb = focal_ref[:, 0:1], focal_ref[:, 1:2]
    one = coef_ref[:, 0:1]
    two = coef_ref[:, LANES - 1:LANES]
    for r in range(rows):
        ids = (me * rows + r) * cols + lax.broadcasted_iota(jnp.int32, (block, cols), 1)
        onehot = (ids == fa).astype(F32) - (ids == fb).astype(F32)
        right = background[r:r + 1, :] + FOCAL_CURRENT * onehot
        sol_ref[:, r, :] = one * q_ref[r] - two * z_ref[r]
        res_ref[:, r, :] = right - one * w_ref[r] + two * y_ref[r]


def on_device(count, cond, nodata, gmask, gval, smask, scur, tinv, focal):
    rows, cols = cond.shape
    pairs = focal.shape[0]
    tiles = cols // LANES
    ext = pairs + EXTRA
    field = jax.ShapeDtypeStruct((rows, ext, cols), F32)
    vm = pl.BlockSpec(memory_space=pltpu.VMEM)
    msg = (2, 2 * pairs + 3 * tiles, LANES)
    others = count - 1
    q, w, z, y, coef = pl.pallas_call(
        functools.partial(krylov_kernel, count),
        out_shape=[field] * 4 + [jax.ShapeDtypeStruct((pairs, LANES), F32)],
        in_specs=[vm] * 8,
        out_specs=[vm] * 5,
        scratch_shapes=[
            pltpu.VMEM((rows, ext, cols), F32),
            pltpu.VMEM((rows, tiles, LANES, 2 * LANES), BF16),
            pltpu.VMEM((rows, 8, cols), F32),
            pltpu.VMEM((2, ext, cols), F32),
            pltpu.VMEM((2, ext, cols), F32),
            pltpu.VMEM(msg, F32),
            pltpu.VMEM(msg, F32),
            pltpu.VMEM((4, ext, LANES), F32),
            pltpu.VMEM((8, LANES), F32),
            pltpu.VMEM((others, 8, LANES), F32),
            pltpu.SemaphoreType.DMA((2,)),
            pltpu.SemaphoreType.DMA((2,)),
            pltpu.SemaphoreType.DMA((2,)),
            pltpu.SemaphoreType.DMA((2,)),
            pltpu.SemaphoreType.DMA((others,)),
            pltpu.SemaphoreType.DMA((others,)),
        ],
        compiler_params=pltpu.CompilerParams(
            collective_id=0, has_side_effects=True, vmem_limit_bytes=36 * 1024 * 1024
        ),
        name="krylov",
    )(cond, nodata, gmask, gval, smask, scur, tinv, focal)

    block = 16 if pairs % 16 == 0 else 8
    fspec = pl.BlockSpec((rows, block, cols), lambda i: (0, i, 0))
    whole = pl.BlockSpec((rows, cols), lambda i: (0, 0))
    ospec = pl.BlockSpec((block, rows, cols), lambda i: (i, 0, 0))
    out = jax.ShapeDtypeStruct((pairs, rows, cols), F32)
    return tuple(pl.pallas_call(
        combine_kernel,
        grid=(pairs // block,),
        out_shape=[out, out],
        in_specs=[
            whole, whole,
            pl.BlockSpec((block, 2), lambda i: (i, 0)),
            pl.BlockSpec((block, LANES), lambda i: (i, 0)),
            fspec, fspec, fspec, fspec,
        ],
        out_specs=[ospec, ospec],
        compiler_params=pltpu.CompilerParams(vmem_limit_bytes=20 * 1024 * 1024),
        name="combine",
    )(smask, scur, focal, coef, q, w, z, y))


def solution(mesh):
    return jax.shard_map(
        functools.partial(on_device, mesh.shape["space"]),
        mesh=mesh,
        in_specs=(
            P(("groups", "space"), None),
            P(("groups", "space"), None),
            P(("groups", "space"), None),
            P(("groups", "space"), None),
            P(("groups", "space"), None),
            P(("groups", "space"), None),
            P(("groups", "space"), None, None, None),
            P(("groups", "rhs"), None),
        ),
        out_specs=(P("rhs", ("groups", "space"), None), P("rhs", ("groups", "space"), None)),
        check_vma=False,
    )
```

time: 106 us -> 42.5 us (0.40)
  Pallas kernels: 0 us -> 33.8 us
  other arithmetic: 27 us -> 0 us
  matrix products: 18.6 us -> 0 us
  blocking collectives: 18.5 us -> 0 us
  starting transfers between devices: 16.3 us -> 0 us
  waiting for transfers between devices: 14.2 us -> 0 us
  local copies, waits for them, and re-layouts: 10.4 us -> 7.5 us
    pallas_call x0 -> x2, Pallas kernels: none -> 33.8 us  [the longest x1 29.3 us: on_device(): pl.pallas_call(functools.partial(krylov_kernel, count), out_shape=[field]...]
    dot_general x2 -> x0, matrix products: 18.6 us -> none  [precondition(): jnp.einsum('rcij,prcj->prci', tile_inverse, blocks, precision=lax.Precisi...]
    psum x2 -> x0, blocking collectives: 18.5 us -> none  [paired_sums(): lax.psum((inner_sum(residual, precond), inner_sum(image, precond)), 'space')]
    ppermute x6 -> x0, starting transfers between devices: 16.3 us -> none  [the longest x3 12.1 us: with_halo(): lax.ppermute(tail, axis, [(i, (i + 1) % count) for i in range(ends)])]
    ppermute x6 -> x0, waiting for transfers between devices: 14.2 us -> none  [the longest x3 8.68 us: with_halo(): lax.ppermute(head, axis, [((i + 1) % count, i) for i in range(ends)])]
    unnamed x16 -> x15, local copies, waits for them, and re-layouts: 0.41 us -> 7.5 us
    concatenate x3 -> x0, other arithmetic: 6.85 us -> none  [with_halo(): jnp.concatenate([lax.ppermute(tail, axis, [(i, (i + 1) % count) for i in...]
    reduce_sum x2 -> x0, other arithmetic: 6.4 us -> none  [inner_sum(): return jnp.sum(first * second, axis=(1, 2))]
  transfers between devices with their start and end apart: 6 -> 0, of which waited for: 4 -> 0; matrix products, arithmetic and copies ran while one was open for 16% -> 0% of each run, Pallas kernels for 0% -> 0%
where the time goes in v1:
time: 42.5 us; the launch traced here: 41.9 us
  Pallas kernels  33.8 us (80%)
  local copies, waits for them, and re-layouts  7.5 us (18%)
  between operations  0.65 us (2%)
    pallas_call x1, Pallas kernels, on_device(): pl.pallas_call(functools.partial(krylov_kernel, count), out_shape=[field]...  29.3 us
    unnamed x15, local copies, waits for them, and re-layouts  7.5 us
    pallas_call x1, Pallas kernels, on_device(): pl.pallas_call(combine_kernel, grid=(pairs // block,), out_shape=[out, ou...  4.43 us

profile of v1, /device:TPU:0, one launch (start us, length us, event | category | flops | bytes accessed | tf_op | source)
XLA Modules:
  0.0 41.9 jit_solution(1637630352279077567)
XLA Ops:
  0.6 0.8 %copy.11.focal_ref = s32[64,2]{1,0:T(8,128)S(1)} copy(s32[64,2]{0,1:T(2,128)} %param.15) | data formatting | bytes 1024 | tf_op args[7]
  1.4 0.0 copy-start
  1.4 2.2 %copy-done = f32[8,8,128,128]{3,2,1,0:T(8,128)S(1)} copy-done((f32[8,8,128,128]{3,2,1,0:T(8,128)S(1)}, f32[8,8,128,128]{3,2,1,0:T(8,128)}, u32[]{:S(2)}) %copy-start) | copy-done | bytes 4194328
  3.6 0.0 copy-start.1
  3.6 0.8 %copy-done.1 = s32[8,1024]{1,0:T(8,128)S(1)} copy-done((s32[8,1024]{1,0:T(8,128)S(1)}, s32[8,1024]{1,0:T(8,128)}, u32[]{:S(2)}) %copy-start.1) | copy-done | bytes 32792
  4.3 0.0 copy-start.2
  4.3 0.8 %copy-done.2 = f32[8,1024]{1,0:T(8,128)S(1)} copy-done((f32[8,1024]{1,0:T(8,128)S(1)}, f32[8,1024]{1,0:T(8,128)}, u32[]{:S(2)}) %copy-start.2) | copy-done | bytes 32792
  5.1 0.0 copy-start.3
  5.1 0.8 %copy-done.3 = f32[8,1024]{1,0:T(8,128)S(1)} copy-done((f32[8,1024]{1,0:T(8,128)S(1)}, f32[8,1024]{1,0:T(8,128)}, u32[]{:S(2)}) %copy-start.3) | copy-done | bytes 32792
  5.9 0.0 copy-start.4
  5.9 0.8 %copy-done.4 = s32[8,1024]{1,0:T(8,128)S(1)} copy-done((s32[8,1024]{1,0:T(8,128)S(1)}, s32[8,1024]{1,0:T(8,128)}, u32[]{:S(2)}) %copy-start.4) | copy-done | bytes 32792
  6.6 0.0 copy-start.5
  6.6 0.8 %copy-done.5 = s32[8,1024]{1,0:T(8,128)S(1)} copy-done((s32[8,1024]{1,0:T(8,128)S(1)}, s32[8,1024]{1,0:T(8,128)}, u32[]{:S(2)}) %copy-start.5) | copy-done | bytes 32792
  7.4 0.0 copy-start.6
  7.4 0.8 %copy-done.6 = f32[8,1024]{1,0:T(8,128)S(1)} copy-done((f32[8,1024]{1,0:T(8,128)S(1)}, f32[8,1024]{1,0:T(8,128)}, u32[]{:S(2)}) %copy-start.6) | copy-done | bytes 32792
  8.1 29.3 %krylov.1 = (f32[8,72,1024]{2,1,0:T(8,128)S(1)}, f32[8,72,1024]{2,1,0:T(8,128)S(1)}, f32[8,72,1024]{2,1,0:T(8,128)S(1)}, f32[8,72,1024]{2,1,0:T(8,128)S(1)}, f32[64,128]{1,0:T(8,128)S(1)}) custom-call(f32[8,1024]{1,0:T(8,128)S(1)} %copy-done.3, s32[8,1024]{1,0:T(8,128)S(1)} %copy-done.4, s32[8,1024]{1,0:T(8,128)S(1)} %copy-done.5, f32[8,1024]{1,0:T(8,128)S(1)} %copy-done.6, ...), custom_call_target="tpu_custom_call" | custom-call | tf_op jit(solution)/shard_map/krylov/pallas_call | solution.py:312
  37.5 4.4 %combine.1 = (f32[64,8,1024]{2,1,0:T(8,128)}, f32[64,8,1024]{2,1,0:T(8,128)}) custom-call(s32[8,1024]{1,0:T(8,128)S(1)} %copy-done.1, f32[8,1024]{1,0:T(8,128)S(1)} %copy-done.2, s32[64,2]{1,0:T(8,128)S(1)} %copy.11.focal_ref, f32[64,128]{1,0:T(8,128)S(1)} %get-tuple-element.7.coef_ref, f32[8,72,1024]{2,1,0:T(8,128)S(1)} %get-tuple-element.8.q_ref, ...), custom_call_target="tpu_custom_call" | custom-call | tf_op jit(solution)/shard_map/combine/pallas_call | solution.py:346
Async XLA Ops:
  1.4 2.2 %copy-start = (f32[8,8,128,128]{3,2,1,0:T(8,128)S(1)}, f32[8,8,128,128]{3,2,1,0:T(8,128)}, u32[]{:S(2)}) copy-start(f32[8,8,128,128]{3,2,1,0:T(8,128)} %t_ref.1) | copy-start | bytes 12582916
  3.6 0.8 %copy-start.1 = (s32[8,1024]{1,0:T(8,128)S(1)}, s32[8,1024]{1,0:T(8,128)}, u32[]{:S(2)}) copy-start(s32[8,1024]{1,0:T(8,128)} %smask_ref.3) | copy-start | bytes 98308
  4.3 0.8 %copy-start.2 = (f32[8,1024]{1,0:T(8,128)S(1)}, f32[8,1024]{1,0:T(8,128)}, u32[]{:S(2)}) copy-start(f32[8,1024]{1,0:T(8,128)} %scur_ref.3) | copy-start | bytes 98308
  5.1 0.8 %copy-start.3 = (f32[8,1024]{1,0:T(8,128)S(1)}, f32[8,1024]{1,0:T(8,128)}, u32[]{:S(2)}) copy-start(f32[8,1024]{1,0:T(8,128)} %cond_ref.1) | copy-start | bytes 98308
  5.9 0.8 %copy-start.4 = (s32[8,1024]{1,0:T(8,128)S(1)}, s32[8,1024]{1,0:T(8,128)}, u32[]{:S(2)}) copy-start(s32[8,1024]{1,0:T(8,128)} %nodata_ref.1) | copy-start | bytes 98308
  6.6 0.8 %copy-start.5 = (s32[8,1024]{1,0:T(8,128)S(1)}, s32[8,1024]{1,0:T(8,128)}, u32[]{:S(2)}) copy-start(s32[8,1024]{1,0:T(8,128)} %gmask_ref.1) | copy-start | bytes 98308
  7.4 0.8 %copy-start.6 = (f32[8,1024]{1,0:T(8,128)S(1)}, f32[8,1024]{1,0:T(8,128)}, u32[]{:S(2)}) copy-start(f32[8,1024]{1,0:T(8,128)} %gval_ref.1) | copy-start | bytes 98308

commit v2 on v1

--- a/solution.py
+++ b/solution.py
@@ -23,14 +23,15 @@
 
 
 def krylov_kernel(
-    count, cond_ref, nodata_ref, gmask_ref, gval_ref, smask_ref, scur_ref, t_ref, focal_ref,
-    q_ref, w_ref, z_ref, y_ref, coef_ref,
-    r0_ref, thl_ref, wts_ref, qhalo_ref, zhalo_ref, msg_ref, got_ref, acc_ref, stat_ref, all_ref,
-    send1, recv1, send2, recv2, send3, recv3,
+    count, cond_hbm, nodata_hbm, gmask_hbm, gval_hbm, smask_hbm, scur_hbm, t_hbm, focal_hbm,
+    r0_ref, q_ref, w_ref, z_ref, y_ref, coef_ref,
+    cond_ref, nodata_ref, gmask_ref, gval_ref, smask_ref, scur_ref, focal_ref, t_ref,
+    thl_ref, wts_ref, qhalo_ref, zhalo_ref, msg_ref, got_ref, acc_ref, stat_ref, all_ref,
+    send1, recv1, send2, recv2, send3, recv3, sem_in, sem_t,
 ):
     rows, cols = cond_ref.shape
     tiles = cols // LANES
-    pairs = focal_ref.shape[0]
+    pairs = focal_ref.shape[1]
     ext = pairs + EXTRA
     groups = ext // 8
     me = lax.axis_index("space")
@@ -42,6 +43,25 @@
             barrier, inc=1, device_id={"space": lax.rem(me + off, count)},
             device_id_type=pl.DeviceIdType.MESH,
         )
+
+    loads = [
+        pltpu.make_async_copy(src, dst, sem_in.at[i])
+        for i, (src, dst) in enumerate((
+            (focal_hbm, focal_ref), (smask_hbm, smask_ref), (scur_hbm, scur_ref),
+            (cond_hbm, cond_ref), (nodata_hbm, nodata_ref), (gmask_hbm, gmask_ref),
+            (gval_hbm, gval_ref),
+        ))
+    ]
+
+    def t_load(r):
+        return pltpu.make_async_copy(t_hbm.at[r], t_ref.at[r], sem_t.at[r])
+
+    for load in loads:
+        load.start()
+    for r in (0, rows - 1, *range(1, rows - 1)):
+        t_load(r).start()
+    for load in loads:
+        load.wait()
 
     valid = (1 - nodata_ref[...]).astype(F32)
     active = cond_ref[...] * valid
@@ -77,17 +97,25 @@
             for i, x in enumerate((dg, nw, sw, ww, ew)):
                 wts_ref[r, i:i + 1, :] = x[r:r + 1, :]
 
-    none = jnp.zeros((1, cols), F32)
-    set_weights(none, none, none, none)
-
     acc_ref[...] = jnp.zeros(acc_ref.shape, F32)
-    fa = jnp.concatenate([focal_ref[:, 0:1], jnp.full((EXTRA, 1), -1, jnp.int32)], 0)
-    fb = jnp.concatenate([focal_ref[:, 1:2], jnp.full((EXTRA, 1), -1, jnp.int32)], 0)
-
-    for r in range(rows):
+    diagonal = lax.broadcasted_iota(jnp.int32, (ext, pairs), 0) == lax.broadcasted_iota(
+        jnp.int32, (ext, pairs), 1)
+    is_pair = lax.broadcasted_iota(jnp.int32, (ext, 1), 0) < pairs
+
+    def column(i):
+        line = jnp.broadcast_to(focal_ref[i:i + 1, :].astype(F32), (ext, pairs))
+        at = jnp.sum(jnp.where(diagonal, line, 0.0), 1, keepdims=True).astype(jnp.int32)
+        return jnp.where(is_pair, at, -1)
+
+    fa, fb = column(0), column(1)
+
+    def right_side(r):
         ids = (me * rows + r) * cols + lax.broadcasted_iota(jnp.int32, (ext, cols), 1)
         onehot = (ids == fa).astype(F32) - (ids == fb).astype(F32)
         r0_ref[r] = background[r:r + 1, :] + FOCAL_CURRENT * onehot
+
+    right_side(0)
+    right_side(rows - 1)
 
     def precond_row(src, dst, r, split):
         for c in range(tiles):
@@ -105,6 +133,8 @@
 
     def precond_inner(src, dst, split):
         def body(r, carry):
+            if split:
+                t_load(r).wait()
             precond_row(src, dst, r, split)
             return carry
         lax.fori_loop(1, rows - 1, body, 0)
@@ -146,8 +176,9 @@
 
     has = (me > 0, me < last)
 
-    precond_row(r0_ref, q_ref, 0, True)
-    precond_row(r0_ref, q_ref, rows - 1, True)
+    for r in (0, rows - 1):
+        t_load(r).wait()
+        precond_row(r0_ref, q_ref, r, True)
 
     tile_a = lax.shift_right_logical(fa[:pairs] & (cols - 1), 7)
     tile_b = lax.shift_right_logical(fb[:pairs] & (cols - 1), 7)
@@ -178,9 +209,12 @@
             got_ref[side] = jnp.zeros(got_ref.shape[1:], F32)
             zhalo_ref[side] = jnp.zeros(zhalo_ref.shape[1:], F32)
 
+    none = jnp.zeros((1, cols), F32)
+    set_weights(none, none, none, none)
+    for r in range(1, rows - 1):
+        right_side(r)
     precond_inner(r0_ref, q_ref, True)
     stencil_inner(q_ref, w_ref, r0_ref, 0)
-    precond_inner(w_ref, z_ref, False)
 
     def done(src, dst, ssem, rsem):
         for side in range(2):
@@ -238,6 +272,7 @@
         def _():
             zcopy(side).start()
 
+    precond_inner(w_ref, z_ref, False)
     stencil_inner(z_ref, y_ref, w_ref, 2)
 
     for side in range(2):
@@ -285,19 +320,33 @@
     coef_ref[...] = jnp.where(lane_p < LANES // 2, first, a0 * a1)
 
 
-def combine_kernel(smask_ref, scur_ref, focal_ref, coef_ref, q_ref, w_ref, z_ref, y_ref, sol_ref, res_ref):
-    rows, block, cols = q_ref.shape
-    me = lax.axis_index("space")
-    background = smask_ref[...].astype(F32) * scur_ref[...]
-    fa, fb = focal_ref[:, 0:1], focal_ref[:, 1:2]
-    one = coef_ref[:, 0:1]
-    two = coef_ref[:, LANES - 1:LANES]
-    for r in range(rows):
-        ids = (me * rows + r) * cols + lax.broadcasted_iota(jnp.int32, (block, cols), 1)
-        onehot = (ids == fa).astype(F32) - (ids == fb).astype(F32)
-        right = background[r:r + 1, :] + FOCAL_CURRENT * onehot
-        sol_ref[:, r, :] = one * q_ref[r] - two * z_ref[r]
-        res_ref[:, r, :] = right - one * w_ref[r] + two * y_ref[r]
+def combine_kernel(coef_ref, r0_ref, q_ref, w_ref, z_ref, y_ref, sol_hbm, res_hbm, sol_ref, res_ref, sem):
+    pairs, rows, cols = sol_ref.shape
+    block = 8
+
+    def out(i, src, dst, k):
+        cut = pl.ds(pl.multiple_of(i * block, block), block)
+        return pltpu.make_async_copy(src.at[cut], dst.at[cut], sem.at[k, i])
+
+    def body(i, carry):
+        cut = pl.ds(pl.multiple_of(i * block, block), block)
+        one = coef_ref[cut, 0:1]
+        two = coef_ref[cut, LANES - 1:LANES]
+        for r in range(rows):
+            sol_ref[cut, r, :] = one * q_ref[r, cut, :] - two * z_ref[r, cut, :]
+            res_ref[cut, r, :] = r0_ref[r, cut, :] - one * w_ref[r, cut, :] + two * y_ref[r, cut, :]
+        out(i, sol_ref, sol_hbm, 0).start()
+        out(i, res_ref, res_hbm, 1).start()
+        return carry
+
+    lax.fori_loop(0, pairs // block, body, 0)
+
+    def finish(i, carry):
+        out(i, sol_ref, sol_hbm, 0).wait()
+        out(i, res_ref, res_hbm, 1).wait()
+        return carry
+
+    lax.fori_loop(0, pairs // block, finish, 0)
 
 
 def on_device(count, cond, nodata, gmask, gval, smask, scur, tinv, focal):
@@ -307,15 +356,24 @@
     ext = pairs + EXTRA
     field = jax.ShapeDtypeStruct((rows, ext, cols), F32)
     vm = pl.BlockSpec(memory_space=pltpu.VMEM)
+    hbm = pl.BlockSpec(memory_space=pltpu.HBM)
     msg = (2, 2 * pairs + 3 * tiles, LANES)
     others = count - 1
-    q, w, z, y, coef = pl.pallas_call(
+    small = (rows, cols)
+    r0, q, w, z, y, coef = pl.pallas_call(
         functools.partial(krylov_kernel, count),
-        out_shape=[field] * 4 + [jax.ShapeDtypeStruct((pairs, LANES), F32)],
-        in_specs=[vm] * 8,
-        out_specs=[vm] * 5,
+        out_shape=[field] * 5 + [jax.ShapeDtypeStruct((pairs, LANES), F32)],
+        in_specs=[hbm] * 8,
+        out_specs=[vm] * 6,
         scratch_shapes=[
-            pltpu.VMEM((rows, ext, cols), F32),
+            pltpu.VMEM(small, F32),
+            pltpu.VMEM(small, jnp.int32),
+            pltpu.VMEM(small, jnp.int32),
+            pltpu.VMEM(small, F32),
+            pltpu.VMEM(small, jnp.int32),
+            pltpu.VMEM(small, F32),
+            pltpu.VMEM((2, pairs), jnp.int32),
+            pltpu.VMEM(tinv.shape, F32),
             pltpu.VMEM((rows, tiles, LANES, 2 * LANES), BF16),
             pltpu.VMEM((rows, 8, cols), F32),
             pltpu.VMEM((2, ext, cols), F32),
@@ -331,32 +389,32 @@
             pltpu.SemaphoreType.DMA((2,)),
             pltpu.SemaphoreType.DMA((others,)),
             pltpu.SemaphoreType.DMA((others,)),
+            pltpu.SemaphoreType.DMA((7,)),
+            pltpu.SemaphoreType.DMA((rows,)),
         ],
         compiler_params=pltpu.CompilerParams(
             collective_id=0, has_side_effects=True, vmem_limit_bytes=36 * 1024 * 1024
         ),
         name="krylov",
-    )(cond, nodata, gmask, gval, smask, scur, tinv, focal)
-
-    block = 16 if pairs % 16 == 0 else 8
-    fspec = pl.BlockSpec((rows, block, cols), lambda i: (0, i, 0))
-    whole = pl.BlockSpec((rows, cols), lambda i: (0, 0))
-    ospec = pl.BlockSpec((block, rows, cols), lambda i: (i, 0, 0))
+    )(*(
+        pltpu.with_memory_space_constraint(x, pltpu.HBM)
+        for x in (cond, nodata, gmask, gval, smask, scur, tinv, focal.T)
+    ))
+
     out = jax.ShapeDtypeStruct((pairs, rows, cols), F32)
     return tuple(pl.pallas_call(
         combine_kernel,
-        grid=(pairs // block,),
         out_shape=[out, out],
-        in_specs=[
-            whole, whole,
-            pl.BlockSpec((block, 2), lambda i: (i, 0)),
-            pl.BlockSpec((block, LANES), lambda i: (i, 0)),
-            fspec, fspec, fspec, fspec,
+        in_specs=[vm] * 6,
+        out_specs=[hbm, hbm],
+        scratch_shapes=[
+            pltpu.VMEM(out.shape, F32),
+            pltpu.VMEM(out.shape, F32),
+            pltpu.SemaphoreType.DMA((2, pairs // 8)),
         ],
-        out_specs=[ospec, ospec],
         compiler_params=pltpu.CompilerParams(vmem_limit_bytes=20 * 1024 * 1024),
         name="combine",
-    )(smask, scur, focal, coef, q, w, z, y))
+    )(coef, r0, q, w, z, y))
 
 
 def solution(mesh):

time: 42.5 us -> 33.8 us (0.80); the launches traced: 41.9 us -> 33.7 us
  local copies, waits for them, and re-layouts: 7.5 us -> 0 us
  Pallas kernels: 33.8 us -> 33 us
    unnamed x15 -> x0, local copies, waits for them, and re-layouts: 7.5 us -> none
    pallas_call x1, Pallas kernels: 4.43 us -> 3.06 us  [on_device(): pl.pallas_call(combine_kernel, out_shape=[out, out], in_specs=[vm] * 6, o...]
    pallas_call x1, Pallas kernels: 29.3 us -> 30 us  [on_device(): pl.pallas_call(functools.partial(krylov_kernel, count), out_shape=[field]...]
where the time goes in v2:
time: 33.8 us; the launch traced here: 33.7 us
  Pallas kernels  33 us (98%)
  between operations  0.64 us (2%)
    pallas_call x1, Pallas kernels, on_device(): pl.pallas_call(functools.partial(krylov_kernel, count), out_shape=[field]...  30 us
    pallas_call x1, Pallas kernels, on_device(): pl.pallas_call(combine_kernel, out_shape=[out, out], in_specs=[vm] * 6, o...  3.06 us

profile of v2, /device:TPU:0, one launch (start us, length us, event | category | flops | bytes accessed | tf_op | source)
XLA Modules:
  0.0 33.7 jit_solution(18193763451989967071)
XLA Ops:
  0.6 30.0 %krylov.1 = (f32[8,72,1024]{2,1,0:T(8,128)S(1)}, f32[8,72,1024]{2,1,0:T(8,128)S(1)}, f32[8,72,1024]{2,1,0:T(8,128)S(1)}, f32[8,72,1024]{2,1,0:T(8,128)S(1)}, f32...) custom-call(f32[8,1024]{1,0:T(8,128)} %cond_hbm.1, s32[8,1024]{1,0:T(8,128)} %nodata_hbm.1, s32[8,1024]{1,0:T(8,128)} %gmask_hbm.1, ...), custom_call_target="tpu_custom_call" | custom-call | tf_op jit(solution)/shard_map/krylov/pallas_call | solution.py:363
  30.6 3.1 %combine.1 = (f32[64,8,1024]{2,1,0:T(8,128)}, f32[64,8,1024]{2,1,0:T(8,128)}) custom-call(f32[64,128]{1,0:T(8,128)S(1)} %get-tuple-element.8.coef_ref, f32[8,72,1024]{2,1,0:T(8,128)S(1)} %get-tuple-element.9.r0_ref, f32[8,72,1024]{2,1,0:T(8,128)S(1)} %get-tuple-element.10.q_ref, f32[8,72,1024]{2,1,0:T(8,128)S(1)} %get-tuple-element.11.w_ref, ...), custom_call_target="tpu_custom_call" | custom-call | tf_op jit(solution)/shard_map/combine/pallas_call | solution.py:405

commit v3 on v2

--- a/solution.py
+++ b/solution.py
@@ -26,7 +26,7 @@
     count, cond_hbm, nodata_hbm, gmask_hbm, gval_hbm, smask_hbm, scur_hbm, t_hbm, focal_hbm,
     r0_ref, q_ref, w_ref, z_ref, y_ref, coef_ref,
     cond_ref, nodata_ref, gmask_ref, gval_ref, smask_ref, scur_ref, focal_ref, t_ref,
-    thl_ref, wts_ref, qhalo_ref, zhalo_ref, msg_ref, got_ref, acc_ref, stat_ref, all_ref,
+    thl_ref, wts_ref, qhalo_ref, zhalo_ref, msg_ref, got_ref, zmsg_ref, zgot_ref, acc_ref, stat_ref, all_ref,
     send1, recv1, send2, recv2, send3, recv3, sem_in, sem_t,
 ):
     rows, cols = cond_ref.shape
@@ -154,7 +154,7 @@
             acc_ref[base, s, :] += fold(left[r, s, :] * ce)
             acc_ref[base + 1, s, :] += fold(ce * out)
             return carry
-        lax.fori_loop(0, groups, body, 0)
+        lax.fori_loop(0, groups, body, 0, unroll=3 if groups % 3 == 0 else 1)
 
     def stencil_inner(src, dst, left, base):
         def body(r, carry):
@@ -182,21 +182,28 @@
 
     tile_a = lax.shift_right_logical(fa[:pairs] & (cols - 1), 7)
     tile_b = lax.shift_right_logical(fb[:pairs] & (cols - 1), 7)
-    for side, r in ((0, 0), (1, rows - 1)):
-        va = q_ref[r, :pairs, 0:LANES]
+    def pack(src, r, dst, side):
+        va = src[r, :pairs, 0:LANES]
         vb = va
         for c in range(1, tiles):
-            x = q_ref[r, :pairs, c * LANES:(c + 1) * LANES]
+            x = src[r, :pairs, c * LANES:(c + 1) * LANES]
             va = jnp.where(tile_a == c, x, va)
             vb = jnp.where(tile_b == c, x, vb)
-        msg_ref[side, 0:pairs, :] = va
-        msg_ref[side, pairs:2 * pairs, :] = vb
+        dst[side, 0:pairs, :] = va
+        dst[side, pairs:2 * pairs, :] = vb
+        for c in range(tiles):
+            at = 2 * pairs + c
+            dst[side, at:at + 1, :] = src[r, pairs:pairs + 1, c * LANES:(c + 1) * LANES]
+
+    for side, r in ((0, 0), (1, rows - 1)):
+        pack(q_ref, r, msg_ref, side)
         for c in range(tiles):
             cut = slice(c * LANES, (c + 1) * LANES)
             at = 2 * pairs + c
-            msg_ref[side, at:at + 1, :] = q_ref[r, pairs:pairs + 1, cut]
             msg_ref[side, at + tiles:at + tiles + 1, :] = active[r:r + 1, cut]
             msg_ref[side, at + 2 * tiles:at + 2 * tiles + 1, :] = valid[r:r + 1, cut]
+            msg_ref[side, at + 3 * tiles:at + 3 * tiles + 1, :] = t_ref[r, c, 0:1, :]
+            msg_ref[side, at + 4 * tiles:at + 4 * tiles + 1, :] = t_ref[r, c, LANES - 1:LANES, :]
 
     pl.semaphore_wait(barrier, last)
     for side in range(2):
@@ -207,7 +214,7 @@
         @pl.when(jnp.logical_not(has[side]))
         def _():
             got_ref[side] = jnp.zeros(got_ref.shape[1:], F32)
-            zhalo_ref[side] = jnp.zeros(zhalo_ref.shape[1:], F32)
+            zgot_ref[side] = jnp.zeros(zgot_ref.shape[1:], F32)
 
     none = jnp.zeros((1, cols), F32)
     set_weights(none, none, none, none)
@@ -250,35 +257,42 @@
     precond_row(w_ref, z_ref, 0, False)
     precond_row(w_ref, z_ref, rows - 1, False)
 
-    def zcopy(side):
-        r = 0 if side == 0 else rows - 1
-        return pltpu.make_async_remote_copy(
-            src_ref=z_ref.at[r], dst_ref=zhalo_ref.at[1 - side],
-            send_sem=send2.at[side], recv_sem=recv2.at[1 - side],
-            device_id={"space": me - 1 if side == 0 else me + 1},
-            device_id_type=pl.DeviceIdType.MESH,
-        )
-
-    def zarrive(side):
-        return pltpu.make_async_remote_copy(
-            src_ref=z_ref.at[0], dst_ref=zhalo_ref.at[side],
-            send_sem=send2.at[1 - side], recv_sem=recv2.at[side],
-            device_id={"space": me - 1 if side == 0 else me + 1},
-            device_id_type=pl.DeviceIdType.MESH,
-        )
+    ends_at = 2 * pairs + tiles
+    lane_e = lax.broadcasted_iota(jnp.int32, (pairs, LANES), 1)
+    for side, r in ((0, 0), (1, rows - 1)):
+        pack(z_ref, r, zmsg_ref, side)
+        ends = jnp.zeros((pairs, LANES), F32)
+        for c in range(tiles):
+            cut = slice(c * LANES, (c + 1) * LANES)
+            diff = w_ref[r, :pairs, cut] - w_ref[r, pairs:pairs + 1, cut]
+            ends = jnp.where(lane_e == c, jnp.broadcast_to(diff[:, 0:1], ends.shape), ends)
+            ends = jnp.where(lane_e == tiles + c, jnp.broadcast_to(diff[:, LANES - 1:], ends.shape), ends)
+        zmsg_ref[side, ends_at:ends_at + pairs, :] = ends
 
     for side in range(2):
         @pl.when(has[side])
         def _():
-            zcopy(side).start()
+            side_copy(zmsg_ref, zgot_ref, send2, recv2, side).start()
 
     precond_inner(w_ref, z_ref, False)
     stencil_inner(z_ref, y_ref, w_ref, 2)
 
+    done(zmsg_ref, zgot_ref, send2, recv2)
     for side in range(2):
-        @pl.when(has[side])
-        def _():
-            zarrive(side).wait_recv()
+        va = zgot_ref[side, 0:pairs, :]
+        vb = zgot_ref[side, pairs:2 * pairs, :]
+        ends = zgot_ref[side, ends_at:ends_at + pairs, :]
+        for c in range(tiles):
+            cut = slice(c * LANES, (c + 1) * LANES)
+            common = zgot_ref[side, 2 * pairs + c:2 * pairs + c + 1, :]
+            at = 2 * pairs + 3 * tiles + c
+            other = (
+                common
+                + ends[:, c:c + 1] * got_ref[side, at:at + 1, :]
+                + ends[:, tiles + c:tiles + c + 1] * got_ref[side, at + tiles:at + tiles + 1, :]
+            )
+            zhalo_ref[side, 0:pairs, cut] = jnp.where(tile_a == c, va, jnp.where(tile_b == c, vb, other))
+            zhalo_ref[side, pairs:ext, cut] = jnp.broadcast_to(common, (EXTRA, LANES))
 
     stencil_ends(z_ref, y_ref, zhalo_ref, w_ref, 2)
 
@@ -300,10 +314,6 @@
 
     for k in range(1, count):
         stat_copy(k - 1, lax.rem(me + k, count), k - 1).start()
-    for side in range(2):
-        @pl.when(has[side])
-        def _():
-            zcopy(side).wait_send()
     for k in range(1, count):
         stat_copy(k - 1, lax.rem(me + k, count), k - 1).wait()
     total = mine
@@ -357,7 +367,8 @@
     field = jax.ShapeDtypeStruct((rows, ext, cols), F32)
     vm = pl.BlockSpec(memory_space=pltpu.VMEM)
     hbm = pl.BlockSpec(memory_space=pltpu.HBM)
-    msg = (2, 2 * pairs + 3 * tiles, LANES)
+    msg = (2, 2 * pairs + 5 * tiles, LANES)
+    zmsg = (2, 3 * pairs + tiles, LANES)
     others = count - 1
     small = (rows, cols)
     r0, q, w, z, y, coef = pl.pallas_call(
@@ -380,6 +391,8 @@
             pltpu.VMEM((2, ext, cols), F32),
             pltpu.VMEM(msg, F32),
             pltpu.VMEM(msg, F32),
+            pltpu.VMEM(zmsg, F32),
+            pltpu.VMEM(zmsg, F32),
             pltpu.VMEM((4, ext, LANES), F32),
             pltpu.VMEM((8, LANES), F32),
             pltpu.VMEM((others, 8, LANES), F32),

time: 33.8 us -> 26.2 us (0.78)
  Pallas kernels: 33 us -> 25.4 us
    pallas_call x1, Pallas kernels: 30 us -> 22.3 us  [on_device(): pl.pallas_call(functools.partial(krylov_kernel, count), out_shape=[field]...]
where the time goes in v3:
time: 26.2 us; the launch traced here: 26 us
  Pallas kernels  25.4 us (97%)
  between operations  0.64 us (2%)
    pallas_call x1, Pallas kernels, on_device(): pl.pallas_call(functools.partial(krylov_kernel, count), out_shape=[field]...  22.3 us
    pallas_call x1, Pallas kernels, on_device(): pl.pallas_call(combine_kernel, out_shape=[out, out], in_specs=[vm] * 6, o...  3.06 us

profile of v3, /device:TPU:0, one launch (start us, length us, event | category | flops | bytes accessed | tf_op | source)
XLA Modules:
  0.0 26.0 jit_solution(5287126664277132151)
XLA Ops:
  0.6 22.3 %krylov.1 = (f32[8,72,1024]{2,1,0:T(8,128)S(1)}, f32[8,72,1024]{2,1,0:T(8,128)S(1)}, f32[8,72,1024]{2,1,0:T(8,128)S(1)}, f32[8,72,1024]{2,1,0:T(8,128)S(1)}, f32...) custom-call(f32[8,1024]{1,0:T(8,128)} %cond_hbm.1, s32[8,1024]{1,0:T(8,128)} %nodata_hbm.1, s32[8,1024]{1,0:T(8,128)} %gmask_hbm.1, ...), custom_call_target="tpu_custom_call" | custom-call | tf_op jit(solution)/shard_map/krylov/pallas_call | solution.py:374
  23.0 3.1 %combine.1 = (f32[64,8,1024]{2,1,0:T(8,128)}, f32[64,8,1024]{2,1,0:T(8,128)}) custom-call(f32[64,128]{1,0:T(8,128)S(1)} %get-tuple-element.8.coef_ref, f32[8,72,1024]{2,1,0:T(8,128)S(1)} %get-tuple-element.9.r0_ref, f32[8,72,1024]{2,1,0:T(8,128)S(1)} %get-tuple-element.10.q_ref, f32[8,72,1024]{2,1,0:T(8,128)S(1)} %get-tuple-element.11.w_ref, ...), custom_call_target="tpu_custom_call" | custom-call | tf_op jit(solution)/shard_map/combine/pallas_call | solution.py:418

commit v4 on v3

--- a/solution.py
+++ b/solution.py
@@ -216,6 +216,7 @@
             got_ref[side] = jnp.zeros(got_ref.shape[1:], F32)
             zgot_ref[side] = jnp.zeros(zgot_ref.shape[1:], F32)
 
+    zhalo_ref[...] = jnp.zeros(zhalo_ref.shape, F32)
     none = jnp.zeros((1, cols), F32)
     set_weights(none, none, none, none)
     for r in range(1, rows - 1):
@@ -276,8 +277,10 @@
 
     precond_inner(w_ref, z_ref, False)
     stencil_inner(z_ref, y_ref, w_ref, 2)
+    stencil_ends(z_ref, y_ref, zhalo_ref, w_ref, 2)
 
     done(zmsg_ref, zgot_ref, send2, recv2)
+    cross = jnp.zeros((pairs, LANES), F32)
     for side in range(2):
         va = zgot_ref[side, 0:pairs, :]
         vb = zgot_ref[side, pairs:2 * pairs, :]
@@ -291,10 +294,12 @@
                 + ends[:, c:c + 1] * got_ref[side, at:at + 1, :]
                 + ends[:, tiles + c:tiles + c + 1] * got_ref[side, at + tiles:at + tiles + 1, :]
             )
-            zhalo_ref[side, 0:pairs, cut] = jnp.where(tile_a == c, va, jnp.where(tile_b == c, vb, other))
-            zhalo_ref[side, pairs:ext, cut] = jnp.broadcast_to(common, (EXTRA, LANES))
-
-    stencil_ends(z_ref, y_ref, zhalo_ref, w_ref, 2)
+            halo = jnp.where(tile_a == c, va, jnp.where(tile_b == c, vb, other))
+            r, kind = ((0, 1), (rows - 1, 2))[side]
+            term = wts_ref[r, kind:kind + 1, cut] * halo
+            y_ref[r, :pairs, cut] -= term
+            cross = cross - z_ref[r, :pairs, cut] * term
+    acc_ref[3, :pairs, :] += cross
 
     lane = lax.broadcasted_iota(jnp.int32, (LANES, LANES), 1)
     table = jnp.zeros((LANES, LANES), F32)

time: 26.2 us -> 26.2 us (level)
  no operation moved by 1% of the time
where the time goes in v4:
time: 26.2 us; the launch traced here: 26 us
  Pallas kernels  25.4 us (97%)
  between operations  0.64 us (2%)
    pallas_call x1, Pallas kernels, on_device(): pl.pallas_call(functools.partial(krylov_kernel, count), out_shape=[field]...  22.3 us
    pallas_call x1, Pallas kernels, on_device(): pl.pallas_call(combine_kernel, out_shape=[out, out], in_specs=[vm] * 6, o...  3.06 us

profile of v4, /device:TPU:0, one launch (start us, length us, event | category | flops | bytes accessed | tf_op | source)
XLA Modules:
  0.0 26.0 jit_solution(14487745233323206992)
XLA Ops:
  0.6 22.3 %krylov.1 = (f32[8,72,1024]{2,1,0:T(8,128)S(1)}, f32[8,72,1024]{2,1,0:T(8,128)S(1)}, f32[8,72,1024]{2,1,0:T(8,128)S(1)}, f32[8,72,1024]{2,1,0:T(8,128)S(1)}, f32...) custom-call(f32[8,1024]{1,0:T(8,128)} %cond_hbm.1, s32[8,1024]{1,0:T(8,128)} %nodata_hbm.1, s32[8,1024]{1,0:T(8,128)} %gmask_hbm.1, ...), custom_call_target="tpu_custom_call" | custom-call | tf_op jit(solution)/shard_map/krylov/pallas_call | solution.py:379
  23.0 3.1 %combine.1 = (f32[64,8,1024]{2,1,0:T(8,128)}, f32[64,8,1024]{2,1,0:T(8,128)}) custom-call(f32[64,128]{1,0:T(8,128)S(1)} %get-tuple-element.8.coef_ref, f32[8,72,1024]{2,1,0:T(8,128)S(1)} %get-tuple-element.9.r0_ref, f32[8,72,1024]{2,1,0:T(8,128)S(1)} %get-tuple-element.10.q_ref, f32[8,72,1024]{2,1,0:T(8,128)S(1)} %get-tuple-element.11.w_ref, ...), custom_call_target="tpu_custom_call" | custom-call | tf_op jit(solution)/shard_map/combine/pallas_call | solution.py:423
